TPU v7x, 128 devices: a whole 4x4x4 slice. The times are simulated.
128 devices in a mesh: scen: 32 (over z, y_lo, x), fac: 4 (over y_hi, core).
Axes of the slice: x: 4, y: 4 (y_hi: 2, y_lo: 2; y = y_hi * 2 + y_lo), z: 4, core: 2. Of those that a mesh axis runs over, the one named last changes fastest.
Arguments:
- scenario_draws: bfloat16 [32768, 4096], P('scen'), may hold values from -6 to 6
- cholesky: bfloat16 [4096, 4096], P('scen', 'fac'), may hold values from -1.5 to 1.5, as said below
- exposures: bfloat16 [4096, 4096], P('fac'), may hold values from -0.09375 to 0.09375
- drift: float32 [4096], P('fac'), may hold values from -3 to 3
Outputs:
- covariance: float32 [4096, 4096], P('scen', 'fac')
- expected: float32 [4096], P('fac')
Inputs may be any that keep to these rules, and one draw needn't show every extreme that they name: cholesky is lower triangular (zero above the diagonal) with diagonal entries of 0.5 to 1.5.
All inputs are finite; a program needn't handle non-finite values.
Results may differ from a plain program's by a relative error of at most 0.0013.
Values may be sent and summed in bfloat16 or wider, within the bound.
No kernel may reach another device: no remote copies, remote signals or barrier semaphores. Data moves between devices by JAX's collectives and lax.ppermute only.
A program may use at most 128 MiB of HBM per device.

v0:
```python
import jax
import jax.numpy as jnp
from jax import lax
from jax.sharding import Mesh
from jax.sharding import PartitionSpec as P

SCEN = ("scen_0", "scen_1", "scen_2")


def in_order(tiles, dim):
    tiles = jnp.moveaxis(tiles, 0, dim)
    shape = tiles.shape
    return tiles.reshape(*shape[:dim], shape[dim] * shape[dim + 1], *shape[dim + 2 :])


def gather_in_order(x, axes, order):
    tiles = x
    for k in order:
        tiles = lax.all_gather(tiles, axes[k])
    done = order[::-1]
    back = [done.index(k) for k in range(len(axes))]
    tiles = tiles.transpose(*back, *range(len(axes), tiles.ndim))
    return tiles.reshape(-1, *x.shape)


def whole_of(x, axes, order, dim):
    return in_order(gather_in_order(x, axes, order), dim)


def from_everyone(x, axis):
    copies = jnp.broadcast_to(x, (lax.axis_size(axis), *x.shape))
    return lax.all_to_all(copies, axis, split_axis=0, concat_axis=0, tiled=True)


def over_copies(x, axis):
    return from_everyone(x, axis).sum(axis=0)


def on_device(scenario_draws, cholesky, exposures, drift):
    count_rows = scenario_draws.shape[0]
    own_desks = exposures.shape[0]
    mixed = jnp.dot(
        scenario_draws, whole_of(cholesky, SCEN, (1, 0, 2), 0), preferred_element_type=jnp.float32
    )
    shocks = (mixed + drift[None, :]).astype(jnp.bfloat16)
    pnl_acc = lax.dot_general(
        lax.all_gather(shocks, "fac", axis=1, tiled=True),
        exposures,
        (((1,), (1,)), ((), ())),
        preferred_element_type=jnp.float32,
    )
    pnl = pnl_acc.astype(jnp.bfloat16)
    gathered = lax.all_gather(pnl, "fac", axis=1, tiled=True)
    desk_total = gathered.shape[1]
    column_sums = over_copies(jnp.sum(gathered, axis=0, dtype=jnp.float32), SCEN)
    scenario_total = count_rows * lax.axis_size(SCEN)
    means = column_sums / scenario_total
    col_means = lax.dynamic_slice_in_dim(means, lax.axis_index("fac") * own_desks, own_desks, 0)
    owned_rows = desk_total // lax.axis_size(SCEN)
    row_start = lax.axis_index(SCEN) * owned_rows
    block = lax.psum_scatter(
        lax.dot_general(
            gathered, pnl, (((0,), (0,)), ((), ())), preferred_element_type=jnp.float32
        ),
        SCEN,
        scatter_dimension=0,
        tiled=True,
    )
    row_means = lax.dynamic_slice_in_dim(means, row_start, owned_rows, 0)
    covariance = (block - scenario_total * row_means[:, None] * col_means[None, :]) / (
        scenario_total - 1
    )
    return (covariance, col_means)


def solution(mesh):
    torus = Mesh(
        mesh.devices.reshape(4, 2, 4, mesh.shape["fac"]), ("scen_0", "scen_1", "scen_2", "fac")
    )
    in_specs = (P(SCEN, None), P(SCEN, "fac"), P("fac", None), P("fac"))
    out_specs = (P(SCEN, "fac"), P("fac"))
    return jax.shard_map(
        on_device, mesh=torus, in_specs=in_specs, out_specs=out_specs, check_vma=False
    )
```

profile of v0, /device:TPU:0, one launch (start us, length us, event | category | flops | bytes accessed | tf_op | source)
XLA Modules:
  0.0 532.6 jit_solution(352595188754719642)
XLA Ops:
  7.2 0.0 all-gather.12.cloned.1.call-start
  7.2 10.6 %all-gather = bf16[256,1024]{1,0:T(8,128)(2,1)} all-gather(bf16[128,1024]{1,0:T(8,128)(2,1)} %param.5), channel_id=2, replica_groups=mesh['scen_0'=4,'scen_1'=2,'scen_2'=4,'fac'=4] {'scen_1'}, dimensions={0}, use_global_device_ids=true | all-gather | bytes 786432 | tf_op jit(solution)/shard_map/all_gather | solution.py:19
  17.8 0.0 all-gather.12.cloned.1.call-update
  17.9 0.0 all-gather.14.cloned.1.call-start
  17.9 33.2 %all-gather.12.cloned.1.call-done = bf16[8,128,1024]{2,1,0:T(8,128)(2,1)} async-done(((bf16[2,128,1024]{2,1,0:T(8,128)(2,1)}), bf16[8,128,1024]{2,1,0:T(8,128)(2,1)}) %all-gather.12.cloned.1.call-update) | async-done | bytes 2097168 | tf_op jit(solution)/shard_map/all_gather | solution.py:19
  51.1 0.0 all-gather.14.cloned.1.call-update
  51.1 0.0 all-gather.8.cloned.1.call-start
  51.2 84.5 %all-gather.14.cloned.1.call-done = bf16[16,2,128,1024]{3,2,1,0:T(8,128)(2,1)} async-done(((bf16[4,2,128,1024]{3,2,1,0:T(8,128)(2,1)}), bf16[16,2,128,1024]{3,2,1,0:T(8,128)(2,1)}) %all-gather.14.cloned.1.call-update) | async-done | bytes 8388624 | tf_op jit(solution)/shard_map/all_gather | solution.py:19
  135.7 0.0 copy-start.1
  135.7 8.2 %copy.9 = bf16[4,2,4,128,1024]{4,3,2,1,0:T(8,128)(2,1)} copy(bf16[4,2,4,128,1024]{4,3,1,0,2:T(8,128)(2,1)} %bitcast.12) | data formatting | bytes 16777216 | tf_op jit(solution)/shard_map/transpose | solution.py:22
  143.9 0.0 copy-done.1
  143.9 14.7 %add_convert_fusion = bf16[1024,1024]{1,0:T(8,128)(2,1)} fusion(f32[1024]{0:T(1024)S(1)} %copy-done.1, bf16[1024,4096]{1,0:T(8,128)(2,1)} %param.4, bf16[4096,1024]{1,0:T(8,128)(2,1)} %bitcast.13), kind=kOutput, calls=%fused_computation.1 | convolution fusion | flops 8592031744 | bytes 18878464 | tf_op jit(solution)/shard_map/dot_general | solution.py:42
  158.6 0.0 all-gather.8.cloned.1.call-update
  158.7 0.0 all-gather.10.cloned.1.call-start
  158.7 63.4 %all-gather.8.cloned.1.call-done = bf16[1024,4096]{1,0:T(8,128)(2,1)} async-done(((bf16[1024,1024]{1,0:T(8,128)(2,1)}), bf16[1024,4096]{1,0:T(8,128)(2,1)}) %all-gather.8.cloned.1.call-update) | async-done | bytes 8388624 | tf_op jit(solution)/shard_map/all_gather | solution.py:47
  222.1 14.8 %convolution_convert_fusion = bf16[1024,1024]{1,0:T(8,128)(2,1)} fusion(bf16[1024,4096]{1,0:T(8,128)(2,1)} %all-gather.8.cloned.1.call-done, bf16[1024,4096]{1,0:T(8,128)(2,1)} %param.6), kind=kOutput, calls=%fused_computation.2 | convolution fusion | flops 8590983168 | bytes 18874368 | tf_op jit(solution)/shard_map/dot_general | solution.py:46
  236.9 0.0 all-gather.10.cloned.1.call-update
  236.9 0.2 reduce-scatter.2.cloned.1.call-start
  237.1 61.6 %all-gather.10.cloned.1.call-done = bf16[1024,4096]{1,0:T(8,128)(2,1)} async-done(((bf16[1024,1024]{1,0:T(8,128)(2,1)}), bf16[1024,4096]{1,0:T(8,128)(2,1)}) %all-gather.10.cloned.1.call-update) | async-done | bytes 8388624 | tf_op jit(solution)/shard_map/all_gather | solution.py:53
  298.8 16.1 %fusion = f32[4096,1024]{1,0:T(8,128)} fusion(bf16[1024,4096]{1,0:T(8,128)(2,1)} %all-gather.10.cloned.1.call-done, bf16[1024,1024]{1,0:T(8,128)(2,1)} %convolution_convert_fusion), kind=kOutput, calls=%fused_computation.6 | convolution fusion | flops 8589934592 | bytes 27262976 | tf_op jit(solution)/shard_map/dot_general | solution.py:62
  314.9 0.0 reduce-scatter.2.cloned.1.call-update
  314.9 4.6 convert_reduce_fusion
  319.5 1.3 broadcast_in_dim.2
  320.7 7.3 %all-to-all-start = ((f32[32,1,4096]{2,1,0:T(1,128)}), f32[32,1,4096]{2,1,0:T(1,128)S(1)}, u32[]{:S(2)}, u32[]{:S(2)}) async-start(f32[32,1,4096]{2,1,0:T(1,128)} %broadcast_in_dim.2), calls=%async_computation.1 | async-start | bytes 1048576 | tf_op jit(solution)/shard_map/all_to_all | solution.py:32
  328.0 17.8 %all-to-all-done = f32[32,1,4096]{2,1,0:T(1,128)S(1)} async-done(((f32[32,1,4096]{2,1,0:T(1,128)}), f32[32,1,4096]{2,1,0:T(1,128)S(1)}, u32[]{:S(2)}, u32[]{:S(2)}) %all-to-all-start) | async-done | bytes 524320 | tf_op jit(solution)/shard_map/all_to_all | solution.py:32
  345.8 0.4 reduce_sum.19
  346.2 0.0 copy-start
  346.2 0.1 dynamic-slice_multiply_fusion
  346.3 177.8 %reduce-scatter.2.cloned.1.call-done = f32[128,1024]{1,0:T(8,128)} async-done(((f32[4096,1024]{1,0:T(8,128)}), f32[128,1024]{1,0:T(8,128)}) %reduce-scatter.2.cloned.1.call-update) | async-done | bytes 524304 | tf_op jit(solution)/shard_map/reduce_scatter | solution.py:61
  524.1 2.0 subtract_multiply_fusion
  526.0 0.0 copy-done
  (2 shorter events, 0.0 us)
Async XLA Ops:
  7.2 43.9 %all-gather.12.cloned.1.call-start = ((), (), s32[]{:S(2)}) async-start(), calls=%async_computation.5 | async-start | bytes 2621440 | tf_op jit(solution)/shard_map/all_gather | solution.py:19
  17.9 117.8 %all-gather.14.cloned.1.call-start = ((), (), s32[]{:S(2)}) async-start(), calls=%async_computation.6 | async-start | bytes 10485760 | tf_op jit(solution)/shard_map/all_gather | solution.py:19
  51.1 171.0 %all-gather.8.cloned.1.call-start = ((), (), s32[]{:S(2)}) async-start(), calls=%async_computation.2 | async-start | bytes 10485760 | tf_op jit(solution)/shard_map/all_gather | solution.py:47
  135.7 8.2 %copy-start.1 = (f32[1024]{0:T(1024)S(1)}, f32[1024]{0:T(1024)}, u32[]{:S(2)}) copy-start(f32[1024]{0:T(1024)} %param.7) | copy-start | bytes 12292
  158.7 140.1 %all-gather.10.cloned.1.call-start = ((), (), s32[]{:S(2)}) async-start(), calls=%async_computation.3 | async-start | bytes 10485760 | tf_op jit(solution)/shard_map/all_gather | solution.py:53
  236.9 287.2 %reduce-scatter.2.cloned.1.call-start = ((), (), s32[]{:S(2)}) async-start(), calls=%async_computation.4 | async-start | bytes 17301504 | tf_op jit(solution)/shard_map/reduce_scatter | solution.py:61
  320.7 25.1 %all-to-all-start = ((f32[32,1,4096]{2,1,0:T(1,128)}), f32[32,1,4096]{2,1,0:T(1,128)S(1)}, u32[]{:S(2)}, u32[]{:S(2)}) async-start(f32[32,1,4096]{2,1,0:T(1,128)} %broadcast_in_dim.2), calls=%async_computation.1 | async-start | bytes 1048576 | tf_op jit(solution)/shard_map/all_to_all | solution.py:32
  346.2 179.8 %copy-start = (f32[1024]{0:T(1024)}, f32[1024]{0:T(1024)S(1)}, u32[]{:S(2)}) copy-start(f32[1024]{0:T(1024)S(1)} %dynamic_slice.7) | copy-start | bytes 12292
Sparse Core Ops, SparseCore 0:
  18.0 33.0 all-gather.11
  52.8 82.8 all-gather.13
  158.8 63.2 all-gather.7
  237.0 61.6 all-gather.9
  315.0 209.0 reduce-scatter.1
where the time goes:
time: 533 us
  waiting for transfers between devices  438 us (82%)
  matrix products  45.6 us (9%)
  between operations  13.8 us (3%)
  blocking collectives  10.6 us (2%)
  local copies, waits for them, and re-layouts  9.51 us (2%)
  starting transfers between devices  7.64 us (1%)
  other arithmetic  6.96 us (1%)
    reduce_scatter x1, waiting for transfers between devices, on_device(): lax.psum_scatter(lax.dot_general(gathered, pnl, (((0,), (0,)), ((), ())),...  178 us
    all_gather x2, waiting for transfers between devices, gather_in_order(): tiles = lax.all_gather(tiles, axes[k])  118 us
    all_gather x1, waiting for transfers between devices, on_device(): lax.all_gather(shocks, 'fac', axis=1, tiled=True)  63.4 us
    all_gather x1, waiting for transfers between devices, on_device(): gathered = lax.all_gather(pnl, 'fac', axis=1, tiled=True)  61.6 us
    all_to_all x1, waiting for transfers between devices, from_everyone(): return lax.all_to_all(copies, axis, split_axis=0, concat_axis=0, tiled=True)  17.8 us
    dot_general x1, matrix products, on_device(): lax.dot_general(gathered, pnl, (((0,), (0,)), ((), ())), preferred_elemen...  16.1 us
    dot_general x1, matrix products, on_device(): lax.dot_general(lax.all_gather(shocks, 'fac', axis=1, tiled=True), exposu...  14.8 us
    dot_general x1, matrix products, on_device(): jnp.dot(scenario_draws, whole_of(cholesky, SCEN, (1, 0, 2), 0), preferred...  14.7 us
  transfers between devices with their start and end apart: 6, of which 6 were waited for; matrix products, arithmetic and copies ran while one was open for 1% of the time, Pallas kernels for 0%

commit v1 on v0

--- a/solution.py
+++ b/solution.py
@@ -44,7 +44,9 @@
     )
     shocks = (mixed + drift[None, :]).astype(jnp.bfloat16)
     pnl_acc = lax.dot_general(
-        lax.all_gather(shocks, "fac", axis=1, tiled=True),
+        jnp.concatenate(
+            lax.all_to_all(jnp.stack([shocks] * lax.axis_size("fac")), "fac", 0, 0), axis=1
+        ),
         exposures,
         (((1,), (1,)), ((), ())),
         preferred_element_type=jnp.float32,

time: 533 us -> 569 us (1.068)
  blocking collectives: 10.6 us -> 109 us
  waiting for transfers between devices: 438 us -> 374 us
    all_to_all x0 -> x1, blocking collectives: none -> 98.7 us  [on_device(): lax.all_to_all(jnp.stack([shocks] * lax.axis_size('fac')), 'fac', 0, 0)]
    all_gather x1 -> x0, waiting for transfers between devices: 63.4 us -> none  [on_device(): lax.all_gather(shocks, 'fac', axis=1, tiled=True)]
  transfers between devices with their start and end apart: 6 -> 5, of which waited for: 6 -> 5; matrix products, arithmetic and copies ran while one was open for 1% -> 1% of each run, Pallas kernels for 0% -> 0%
where the time goes in v1:
time: 569 us; the launch traced here: 568 us
  waiting for transfers between devices  374 us (66%)
  blocking collectives  109 us (19%)
  matrix products  43.2 us (8%)
  between operations  13.8 us (2%)
  local copies, waits for them, and re-layouts  13.5 us (2%)
  starting transfers between devices  7.59 us (1%)
  other arithmetic  6.96 us (1%)
    reduce_scatter x1, waiting for transfers between devices, on_device(): lax.psum_scatter(lax.dot_general(gathered, pnl, (((0,), (0,)), ((), ())),...  178 us
    all_gather x2, waiting for transfers between devices, gather_in_order(): tiles = lax.all_gather(tiles, axes[k])  118 us
    all_to_all x1, blocking collectives, on_device(): lax.all_to_all(jnp.stack([shocks] * lax.axis_size('fac')), 'fac', 0, 0)  98.7 us
    all_gather x1, waiting for transfers between devices, on_device(): gathered = lax.all_gather(pnl, 'fac', axis=1, tiled=True)  60.8 us
    all_to_all x1, waiting for transfers between devices, from_everyone(): return lax.all_to_all(copies, axis, split_axis=0, concat_axis=0, tiled=True)  17.8 us
    dot_general x1, matrix products, on_device(): lax.dot_general(gathered, pnl, (((0,), (0,)), ((), ())), preferred_elemen...  16.2 us
    dot_general x1, matrix products, on_device(): jnp.dot(scenario_draws, whole_of(cholesky, SCEN, (1, 0, 2), 0), preferred...  14.7 us
    dot_general x1, matrix products, on_device(): lax.dot_general(jnp.concatenate(lax.all_to_all(jnp.stack([shocks] * lax.a...  12.3 us
  transfers between devices with their start and end apart: 5, of which 5 were waited for; matrix products, arithmetic and copies ran while one was open for 1% of the time, Pallas kernels for 0%

profile of v1, /device:TPU:0, one launch (start us, length us, event | category | flops | bytes accessed | tf_op | source)
XLA Modules:
  0.0 568.4 jit_solution(17965379266684886791)
XLA Ops:
  7.2 0.0 all-gather.9.cloned.1.call-start
  7.2 10.6 %all-gather = bf16[256,1024]{1,0:T(8,128)(2,1)} all-gather(bf16[128,1024]{1,0:T(8,128)(2,1)} %param.5), channel_id=2, replica_groups=mesh['scen_0'=4,'scen_1'=2,'scen_2'=4,'fac'=4] {'scen_1'}, dimensions={0}, use_global_device_ids=true | all-gather | bytes 786432 | tf_op jit(solution)/shard_map/all_gather | solution.py:19
  17.8 0.0 all-gather.9.cloned.1.call-update
  17.9 0.0 all-gather.11.cloned.1.call-start
  17.9 33.2 %all-gather.9.cloned.1.call-done = bf16[8,128,1024]{2,1,0:T(8,128)(2,1)} async-done(((bf16[2,128,1024]{2,1,0:T(8,128)(2,1)}), bf16[8,128,1024]{2,1,0:T(8,128)(2,1)}) %all-gather.9.cloned.1.call-update) | async-done | bytes 2097168 | tf_op jit(solution)/shard_map/all_gather | solution.py:19
  51.1 0.0 all-gather.11.cloned.1.call-update
  51.1 0.0 all-gather.7.cloned.1.call-start
  51.2 84.5 %all-gather.11.cloned.1.call-done = bf16[16,2,128,1024]{3,2,1,0:T(8,128)(2,1)} async-done(((bf16[4,2,128,1024]{3,2,1,0:T(8,128)(2,1)}), bf16[16,2,128,1024]{3,2,1,0:T(8,128)(2,1)}) %all-gather.11.cloned.1.call-update) | async-done | bytes 8388624 | tf_op jit(solution)/shard_map/all_gather | solution.py:19
  135.7 0.0 copy-start.1
  135.7 8.2 %copy.13 = bf16[4,2,4,128,1024]{4,3,2,1,0:T(8,128)(2,1)} copy(bf16[4,2,4,128,1024]{4,3,1,0,2:T(8,128)(2,1)} %bitcast.15) | data formatting | bytes 16777216 | tf_op jit(solution)/shard_map/transpose | solution.py:22
  143.9 0.0 copy-done.1
  143.9 14.7 %add_convert_fusion = bf16[1024,1024]{1,0:T(8,128)(2,1)} fusion(f32[1024]{0:T(1024)S(1)} %copy-done.1, bf16[1024,4096]{1,0:T(8,128)(2,1)} %param.4, bf16[4096,1024]{1,0:T(8,128)(2,1)} %bitcast.16), kind=kOutput, calls=%fused_computation.1 | convolution fusion | flops 8592031744 | bytes 18878464 | tf_op jit(solution)/shard_map/dot_general | solution.py:42
  158.6 2.9 copy.14
  161.5 1.2 stack.2
  162.7 98.7 %all_to_all.11 = bf16[4,1024,1024]{1,2,0:T(8,128)(2,1)S(1)} all-to-all(bf16[4,1024,1024]{1,2,0:T(8,128)(2,1)S(1)} %stack.2), channel_id=1, replica_groups=mesh['scen_0'=4,'scen_1'=2,'scen_2'=4,'fac'=4] {'fac'}, dimensions={0} | all-to-all | bytes 16777216 | tf_op jit(solution)/shard_map/all_to_all | solution.py:48
  261.3 12.3 %convolution_convert_fusion = bf16[1024,1024]{1,0:T(8,128)(2,1)} fusion(bf16[1024,4096]{0,1:T(8,128)(2,1)S(1)} %bitcast.17, bf16[1024,4096]{1,0:T(8,128)(2,1)} %param.6), kind=kOutput, calls=%fused_computation.2 | convolution fusion | flops 8590983168 | bytes 18874368 | tf_op jit(solution)/shard_map/dot_general | solution.py:46
  273.7 0.0 all-gather.7.cloned.1.call-update
  273.7 0.2 reduce-scatter.2.cloned.1.call-start
  273.9 60.8 %all-gather.7.cloned.1.call-done = bf16[1024,4096]{1,0:T(8,128)(2,1)} async-done(((bf16[1024,1024]{1,0:T(8,128)(2,1)}), bf16[1024,4096]{1,0:T(8,128)(2,1)}) %all-gather.7.cloned.1.call-update) | async-done | bytes 8388624 | tf_op jit(solution)/shard_map/all_gather | solution.py:55
  334.7 16.2 %fusion = f32[4096,1024]{1,0:T(8,128)} fusion(bf16[1024,4096]{1,0:T(8,128)(2,1)} %all-gather.7.cloned.1.call-done, bf16[1024,1024]{1,0:T(8,128)(2,1)} %convolution_convert_fusion), kind=kOutput, calls=%fused_computation.6 | convolution fusion | flops 8589934592 | bytes 27262976 | tf_op jit(solution)/shard_map/dot_general | solution.py:64
  350.9 0.0 reduce-scatter.2.cloned.1.call-update
  350.9 4.6 convert_reduce_fusion
  355.5 1.3 broadcast_in_dim.2
  356.7 7.3 %all-to-all-start.1 = ((f32[32,1,4096]{2,1,0:T(1,128)}), f32[32,1,4096]{2,1,0:T(1,128)S(1)}, u32[]{:S(2)}, u32[]{:S(2)}) async-start(f32[32,1,4096]{2,1,0:T(1,128)} %broadcast_in_dim.2), calls=%async_computation.2 | async-start | bytes 1048576 | tf_op jit(solution)/shard_map/all_to_all | solution.py:32
  364.0 17.8 %all-to-all-done.1 = f32[32,1,4096]{2,1,0:T(1,128)S(1)} async-done(((f32[32,1,4096]{2,1,0:T(1,128)}), f32[32,1,4096]{2,1,0:T(1,128)S(1)}, u32[]{:S(2)}, u32[]{:S(2)}) %all-to-all-start.1) | async-done | bytes 524320 | tf_op jit(solution)/shard_map/all_to_all | solution.py:32
  381.8 0.4 reduce_sum.19
  382.2 0.0 copy-start
  382.2 0.1 dynamic-slice_multiply_fusion
  382.3 177.7 %reduce-scatter.2.cloned.1.call-done = f32[128,1024]{1,0:T(8,128)} async-done(((f32[4096,1024]{1,0:T(8,128)}), f32[128,1024]{1,0:T(8,128)}) %reduce-scatter.2.cloned.1.call-update) | async-done | bytes 524304 | tf_op jit(solution)/shard_map/reduce_scatter | solution.py:63
  559.9 2.0 subtract_multiply_fusion
  561.9 0.0 copy-done
  (2 shorter events, 0.0 us)
Async XLA Ops:
  7.2 43.9 %all-gather.9.cloned.1.call-start = ((), (), s32[]{:S(2)}) async-start(), calls=%async_computation.5 | async-start | bytes 2621440 | tf_op jit(solution)/shard_map/all_gather | solution.py:19
  17.9 117.8 %all-gather.11.cloned.1.call-start = ((), (), s32[]{:S(2)}) async-start(), calls=%async_computation.6 | async-start | bytes 10485760 | tf_op jit(solution)/shard_map/all_gather | solution.py:19
  51.1 283.6 %all-gather.7.cloned.1.call-start = ((), (), s32[]{:S(2)}) async-start(), calls=%async_computation.3 | async-start | bytes 10485760 | tf_op jit(solution)/shard_map/all_gather | solution.py:55
  135.7 8.2 %copy-start.1 = (f32[1024]{0:T(1024)S(1)}, f32[1024]{0:T(1024)}, u32[]{:S(2)}) copy-start(f32[1024]{0:T(1024)} %param.7) | copy-start | bytes 12292
  273.7 286.2 %reduce-scatter.2.cloned.1.call-start = ((), (), s32[]{:S(2)}) async-start(), calls=%async_computation.4 | async-start | bytes 17301504 | tf_op jit(solution)/shard_map/reduce_scatter | solution.py:63
  356.7 25.1 %all-to-all-start.1 = ((f32[32,1,4096]{2,1,0:T(1,128)}), f32[32,1,4096]{2,1,0:T(1,128)S(1)}, u32[]{:S(2)}, u32[]{:S(2)}) async-start(f32[32,1,4096]{2,1,0:T(1,128)} %broadcast_in_dim.2), calls=%async_computation.2 | async-start | bytes 1048576 | tf_op jit(solution)/shard_map/all_to_all | solution.py:32
  382.2 179.7 %copy-start = (f32[1024]{0:T(1024)}, f32[1024]{0:T(1024)S(1)}, u32[]{:S(2)}) copy-start(f32[1024]{0:T(1024)S(1)} %dynamic_slice.7) | copy-start | bytes 12292
Sparse Core Ops, SparseCore 0:
  18.0 33.0 all-gather.8
  52.7 82.8 all-gather.10
  273.8 60.8 all-gather.6
  351.0 208.8 reduce-scatter.1
